TPU v7x, 32 devices: a whole 2x2x4 slice. The times are simulated.
32 devices in a mesh: section: 4 (over y, core), expert: 2 (over x), tensor: 4 (over z).
Axes of the slice: x: 2, y: 2, z: 4, core: 2. Of those that a mesh axis runs over, the one named last changes fastest.
Arguments:
- branch_weights: bfloat16 [2, 8192, 8192], P('expert', ('section', 'tensor')), may hold values from -0.125 to 0.125
- branch_gains: float32 [2, 8192], P('expert', ('section', 'tensor')), may hold values from 0.1 to 1.9
- column_order: int32 [2, 8192], P('expert'), may hold values from 0 to 8191, each once within a row
- layer_order: int32 [4], replicated, may hold values from 0 to 3, each once
- probe_seeds: int32 [1024], replicated, may hold values from 1 to 32767
Outputs:
- expert_weights: bfloat16 [2, 8192, 8192], P('expert', None, ('section', 'tensor'))
- checksum: float32 [2, 1024, 8192], P('expert', None, ('section', 'tensor'))
- fingerprint: float32 [2, 1024], P('expert')
- shared_gain: float32 [8192], replicated
Inputs may be any that keep to these rules, and one draw needn't show every extreme that they name: Each row of column_order names every hidden unit once. layer_order names every layer once.
All inputs are finite; a program needn't handle non-finite values.
Results may differ from a plain program's by a relative error of at most 0.0034.
Values may be sent and summed in bfloat16 or wider, within the bound.
A program may use at most 64 MiB of HBM per device.

v0:
```python
import functools

import jax
import jax.numpy as jnp
from jax import lax
from jax.experimental import pallas as pl
from jax.experimental.pallas import tpu as pltpu
from jax.sharding import PartitionSpec as P

MESH = pl.DeviceIdType.MESH


def probe_values(products):
    folded = (products >> 16) * 15 + (products & 65535)
    hashed = jnp.where(folded >= 65521, folded - 65521, folded)
    digits = (hashed >> 9) + (hashed & 511)
    digits = jnp.where(digits >= 511, digits - 511, digits)
    return (digits - 255).astype(jnp.float32) * (1.0 / 256.0)


def exchange(
    n_section, n_expert, n_tensor, layers,
    order_s, w_hbm, gains_ref, cols_ref, seeds_ref,
    arrived, sums_ref, print_ref, means_ref,
    w, staged, acc, onehot, scale, print_acc, seed_col, probes, gains, parts,
    w_sem, send_sem, recv_sem, gain_send, gain_recv, mean_send, mean_recv,
    part_send, part_recv,
):
    section, expert, tensor = (lax.axis_index(a) for a in ("section", "expert", "tensor"))
    groups = n_section * n_tensor
    me = section * n_tensor + tensor
    rows, width = w.shape
    cols = width // groups
    n_probes = seed_col.shape[0]
    deep = onehot.shape[0]
    n_deep = width // deep
    per_layer = groups // layers
    half = n_tensor // 2 if n_tensor % 2 == 0 else n_tensor
    sides = n_tensor // half

    def partner(k, sign):
        m, cross = k // sides, (k + 1) % sides
        j = cross * (m // n_section % half) + (1 - cross) * ((m + 1) % half)
        q = cross * (m % n_section) + (1 - cross) * ((m + 1) // half % n_section)
        i = q if n_section % 2 else q % 2 * (n_section // 2) + q // 2
        t = ((tensor // half + cross) % sides) * half + (tensor % half + sign * j + half) % half
        return (section + sign * i + n_section) % n_section, t

    def remote(src, dst, send, recv, k):
        s, t = partner(k, 1)
        return pltpu.make_async_remote_copy(
            src_ref=src, dst_ref=dst, send_sem=send.at[k], recv_sem=recv.at[k],
            device_id={"section": s, "tensor": t}, device_id_type=MESH)

    def block_copy(k):
        s, t = partner(k, 1)
        return remote(staged.at[s * n_tensor + t], arrived.at[me], send_sem, recv_sem, k)

    def mean_copy(k):
        return remote(means_ref.at[me], means_ref.at[me], mean_send, mean_recv, k)

    def part_copy(k):
        return remote(parts.at[me], parts.at[me], part_send, part_recv, k)

    def gain_copy(j):
        return pltpu.make_async_remote_copy(
            src_ref=gains_ref, dst_ref=gains.at[expert], send_sem=gain_send.at[j],
            recv_sem=gain_recv.at[j], device_id={"expert": (expert + j + 1) % n_expert},
            device_id_type=MESH)

    def w_copy(c):
        at = pl.ds(pl.multiple_of(c * deep, deep), deep)
        return pltpu.make_async_copy(w_hbm.at[0, :, at], w.at[:, at], w_sem.at[c])

    @pl.loop(0, n_deep)
    def _(c):
        w_copy(c).start()

    barrier = pltpu.get_barrier_semaphore()

    @pl.loop(0, groups - 1)
    def _(k):
        s, t = partner(k, 1)
        pl.semaphore_signal(
            barrier, inc=1, device_id={"section": s, "tensor": t}, device_id_type=MESH)

    @pl.loop(0, n_expert - 1)
    def _(j):
        pl.semaphore_signal(
            barrier, inc=1, device_id={"expert": (expert + j + 1) % n_expert},
            device_id_type=MESH)

    print_acc[...] = jnp.zeros_like(print_acc)
    pl.semaphore_wait(barrier, groups - 1 + n_expert - 1)

    @pl.loop(0, n_expert - 1)
    def _(j):
        gain_copy(j).start()

    @pl.loop(0, groups)
    def _(k):
        s, t = partner(k, 1)
        g = s * n_tensor + t
        at = pl.ds(pl.multiple_of(g * cols, cols), cols)
        wanted = cols_ref[:, at]
        acc[...] = jnp.zeros_like(acc)

        @pl.loop(0, n_deep)
        def _(c):
            @pl.when(k == 0)
            def _():
                w_copy(c).wait()

            ids = lax.broadcasted_iota(jnp.int32, (deep, cols), 0)
            onehot[...] = jnp.where(ids == wanted - c * deep, 1.0, 0.0).astype(jnp.bfloat16)
            acc[...] += jnp.dot(
                w[:, pl.ds(pl.multiple_of(c * deep, deep), deep)], onehot[...],
                preferred_element_type=jnp.float32)

        @pl.when(k == 0)
        def _():
            own = gains_ref[...]
            gains[expert] = own

            @pl.loop(0, n_expert - 1)
            def _(j):
                gain_copy(j).wait()

            total = gains[0]
            for e in range(1, n_expert):
                total = total + gains[e]
            mean = total / n_expert
            means_ref[me] = mean
            scale[...] = jnp.broadcast_to(own / mean, (128, rows)).T

        column_ids = g * cols + lax.broadcasted_iota(jnp.int32, (1, cols), 1)
        column_probe = probe_values(7919 * (column_ids + 1))
        for c in range(cols // 128):
            part = slice(c * 128, (c + 1) * 128)
            block = (acc[:, part] * scale[...]).astype(jnp.bfloat16)
            staged[g, :, part] = block
            print_acc[...] += block.astype(jnp.float32) * column_probe[:, part]

        @pl.when(k < groups - 1)
        def _():
            block_copy(k).start()

    @pl.loop(0, groups - 1)
    def _(k):
        mean_copy(k).start()

    sums_ref[...] = jnp.zeros_like(sums_ref)
    seeds = seeds_ref[...]
    seed_col[...] = jnp.broadcast_to(
        seeds.astype(jnp.float32), (128, n_probes)).T.astype(jnp.int32)

    def first_row(g):
        return order_s[g // per_layer] * (rows * per_layer) + (g % per_layer) * rows

    totals = jnp.sum(print_acc[...], axis=1, keepdims=True)
    row_ids = first_row(me) + lax.broadcasted_iota(jnp.int32, (rows, 128), 0)
    for c in range(n_probes // 128):
        part = slice(c * 128, (c + 1) * 128)
        values = probe_values(seeds[:, part] * (row_ids + 1))
        parts[me, :, part] = jnp.sum(values * totals, axis=0, keepdims=True)

    @pl.loop(0, groups - 1)
    def _(k):
        part_copy(k).start()

    def sketch(k, block):
        s, t = partner(k, -1)
        g = s * n_tensor + t
        first = first_row(g) + 1
        chunk = min(64, n_probes)

        @pl.loop(0, n_probes // chunk)
        def _(r):
            at = pl.ds(pl.multiple_of(r * chunk, chunk), chunk)
            for c in range(rows // 128):
                ids = first + c * 128 + lax.broadcasted_iota(jnp.int32, (1, 128), 1)
                probes[at, c * 128:(c + 1) * 128] = probe_values(
                    seed_col[at, :] * ids).astype(jnp.bfloat16)

        sums_ref[...] += jnp.dot(probes[...], block, preferred_element_type=jnp.float32)

    arrived[me] = staged[me]
    sketch(groups - 1, staged[me])

    @pl.loop(0, groups - 1)
    def _(k):
        s, t = partner(k, -1)
        g = s * n_tensor + t
        block_copy(k).wait_recv()
        sketch(k, arrived[g])

    @pl.loop(0, groups - 1)
    def _(k):
        part_copy(k).wait()
        mean_copy(k).wait()

    printed = parts[0]
    for g in range(1, groups):
        printed = printed + parts[g]
    print_ref[...] = printed * width ** -0.5

    @pl.loop(0, groups - 1)
    def _(k):
        block_copy(k).wait_send()


def place(order_s, blocks_ref, sums_ref, print_ref, means_ref,
          weights_out, sums_out, print_out, means_out, block_sem, mean_sem, flat_sem):
    groups = blocks_ref.shape[0]
    per_layer = groups // order_s.shape[0]

    def copies(g):
        to = order_s[g // per_layer] * per_layer + g % per_layer
        return (pltpu.make_async_copy(blocks_ref.at[g], weights_out.at[to], block_sem.at[g]),
                pltpu.make_async_copy(means_ref.at[g], means_out.at[to], mean_sem.at[g]))

    flat = (pltpu.make_async_copy(sums_ref, sums_out, flat_sem.at[0]),
            pltpu.make_async_copy(print_ref, print_out, flat_sem.at[1]))

    @pl.loop(0, groups)
    def _(g):
        for copy in copies(g):
            copy.start()

    for copy in flat:
        copy.start()

    @pl.loop(0, groups)
    def _(g):
        for copy in copies(g):
            copy.wait()

    for copy in flat:
        copy.wait()


def local(n_section, n_expert, n_tensor, branch_weights, branch_gains, column_order,
          layer_order, probe_seeds):
    _, rows, width = branch_weights.shape
    groups = n_section * n_tensor
    cols = width // groups
    layers = layer_order.shape[0]
    n_probes = probe_seeds.shape[0]
    per_layer = groups // layers
    deep = min(1024, width)
    f32, bf16 = jnp.float32, jnp.bfloat16
    vmem = pl.BlockSpec(memory_space=pltpu.VMEM)
    hbm = pl.BlockSpec(memory_space=pl.ANY)
    dma = pltpu.SemaphoreType.DMA
    arrived, sums, printed, means = pl.pallas_call(
        functools.partial(exchange, n_section, n_expert, n_tensor, layers),
        out_shape=(
            jax.ShapeDtypeStruct((groups, rows, cols), bf16),
            jax.ShapeDtypeStruct((n_probes, cols), f32),
            jax.ShapeDtypeStruct((1, n_probes), f32),
            jax.ShapeDtypeStruct((groups, 1, rows), f32),
        ),
        in_specs=[pl.BlockSpec(memory_space=pltpu.SMEM), hbm, vmem, vmem, vmem],
        out_specs=(vmem, vmem, vmem, vmem),
        scratch_shapes=[
            pltpu.VMEM((rows, width), bf16),
            pltpu.VMEM((groups, rows, cols), bf16),
            pltpu.VMEM((rows, cols), f32),
            pltpu.VMEM((deep, cols), bf16),
            pltpu.VMEM((rows, 128), f32),
            pltpu.VMEM((rows, 128), f32),
            pltpu.VMEM((n_probes, 128), jnp.int32),
            pltpu.VMEM((n_probes, rows), bf16),
            pltpu.VMEM((n_expert, 1, rows), f32),
            pltpu.VMEM((groups, 1, n_probes), f32),
            dma((width // deep,)), dma((groups,)), dma((groups,)),
            dma((n_expert,)), dma((n_expert,)), dma((groups,)), dma((groups,)),
            dma((groups,)), dma((groups,)),
        ],
        compiler_params=pltpu.CompilerParams(
            collective_id=0, has_side_effects=True, vmem_limit_bytes=40 * 2 ** 20),
        name="exchange",
    )(layer_order, branch_weights, branch_gains, column_order, probe_seeds.reshape(1, n_probes))

    weights, sums, printed, means = pl.pallas_call(
        place,
        in_specs=[pl.BlockSpec(memory_space=pltpu.SMEM), vmem, vmem, vmem, vmem],
        out_specs=(hbm, hbm, hbm, hbm),
        scratch_shapes=[dma((groups,)), dma((groups,)), dma((2,))],
        out_shape=(
            jax.ShapeDtypeStruct((groups, rows, cols), bf16),
            jax.ShapeDtypeStruct((n_probes, cols), f32),
            jax.ShapeDtypeStruct((1, n_probes), f32),
            jax.ShapeDtypeStruct((groups, 1, rows), f32),
        ),
        compiler_params=pltpu.CompilerParams(
            has_side_effects=True, vmem_limit_bytes=16 * 2 ** 20),
        name="place",
    )(layer_order, arrived, sums, printed, means)
    return (weights.reshape(1, groups * rows, cols), sums[None], printed,
            means.reshape(groups * rows))


def solution(mesh):
    sizes = mesh.shape
    return jax.shard_map(
        functools.partial(local, sizes["section"], sizes["expert"], sizes["tensor"]),
        mesh=mesh,
        in_specs=(
            P("expert", ("section", "tensor"), None),
            P("expert", ("section", "tensor")),
            P("expert", None),
            P(),
            P(),
        ),
        out_specs=(
            P("expert", None, ("section", "tensor")),
            P("expert", None, ("section", "tensor")),
            P("expert", None),
            P(),
        ),
        check_vma=False,
    )
```

profile of v0, /device:TPU:9, one launch (start us, length us, event | category | flops | bytes accessed | tf_op | source)
XLA Modules:
  0.0 206.0 jit_solution(8092373129259360762)
XLA Ops:
  0.6 0.0 copy-start
  0.6 0.7 copy-done
  1.4 0.0 copy-start.1
  1.4 0.7 copy-done.1
  2.1 0.0 copy-start.2
  2.1 0.7 copy-done.2
  2.8 0.0 copy-start.3
  2.8 0.7 copy-done.3
  3.4 197.7 %exchange.1 = (bf16[16,512,512]{2,1,0:T(8,128)(2,1)S(1)}, f32[1024,512]{1,0:T(8,128)S(1)}, f32[1,1024]{1,0:T(1,128)S(1)}, f32[16,1,512]{2,1,0:T(1,128)S(1)}) custom-call(s32[4]{0:T(128)S(1)} %copy-done.3, bf16[1,512,8192]{2,1,0:T(8,128)(2,1)} %w_hbm.1, f32[1,512]{1,0:T(1,128)S(1)} %copy-done.2, s32[1,8192]{1,0:T(1,128)S(1)} %copy-done, s32[1,1024]{1,0:T(1,128)S(1)} %bitcast.4), custom_call_target="tpu_custom_call" | custom-call | tf_op jit(solution)/shard_map/exchange/pallas_call | solution.py:255
  201.2 4.9 %place.1 = (bf16[16,512,512]{2,1,0:T(8,128)(2,1)}, f32[1024,512]{1,0:T(8,128)}, f32[1,1024]{1,0:T(1,128)}, f32[16,1,512]{2,1,0:T(1,128)}) custom-call(s32[4]{0:T(128)S(1)} %copy-done.3, bf16[16,512,512]{2,1,0:T(8,128)(2,1)S(1)} %get-tuple-element.12.blocks_ref, f32[1024,512]{1,0:T(8,128)S(1)} %get-tuple-element.13.sums_ref, ...), custom_call_target="tpu_custom_call" | custom-call | tf_op jit(solution)/shard_map/place/pallas_call | solution.py:285
Async XLA Ops:
  0.6 0.8 copy-start
  1.4 0.7 copy-start.1
  2.1 0.7 copy-start.2
  2.8 0.7 copy-start.3
where the time goes:
time: 207 us; the launch traced here: 206 us
  Pallas kernels  203 us (98%)
  local copies, waits for them, and re-layouts  2.77 us (1%)
    pallas_call x1, Pallas kernels, local(): pl.pallas_call(functools.partial(exchange, n_section, n_expert, n_tensor,...  198 us
    pallas_call x1, Pallas kernels, local(): pl.pallas_call(place, in_specs=[pl.BlockSpec(memory_space=pltpu.SMEM), vm...  4.87 us

commit v1 on v0

v1 whole, which is shorter than its diff:
```python
import functools

import jax
import jax.numpy as jnp
from jax import lax
from jax.experimental import pallas as pl
from jax.experimental.pallas import tpu as pltpu
from jax.sharding import PartitionSpec as P

MESH = pl.DeviceIdType.MESH
LATE = 2


def probe_values(products):
    folded = (products >> 16) * 15 + (products & 65535)
    hashed = jnp.where(folded >= 65521, folded - 65521, folded)
    digits = (hashed >> 9) + (hashed & 511)
    digits = jnp.where(digits >= 511, digits - 511, digits)
    return (digits - 255).astype(jnp.float32) * (1.0 / 256.0)


def partner_of(n_section, n_tensor, section, tensor, k, sign):
    half = n_tensor // 2 if n_tensor % 2 == 0 else n_tensor
    sides = n_tensor // half
    m, cross = k // sides, (k + 1) % sides
    j = cross * (m // n_section % half) + (1 - cross) * ((m + 1) % half)
    q = cross * (m % n_section) + (1 - cross) * ((m + 1) // half % n_section)
    i = q if n_section % 2 else q % 2 * (n_section // 2) + q // 2
    t = ((tensor // half + cross) % sides) * half + (tensor % half + sign * j + half) % half
    return (section + sign * i + n_section) % n_section, t


def exchange(
    n_section, n_expert, n_tensor, layers, late,
    order_hbm, w_hbm, gains_hbm, cols_hbm, seeds_hbm,
    arrived, sums_ref, print_ref, means_ref, late_probes, order_ref,
    w, staged, acc, onehot, scale, print_acc, seed_col, probes, gains, parts,
    cols_ref, seeds_ref, order_s, own_scale, first_scale,
    w_sem, send_sem, recv_sem, gain_send, gain_recv, mean_send, mean_recv,
    part_send, part_recv, piece_send, piece_recv, scale_sem, small_sem,
):
    section, expert, tensor = (lax.axis_index(a) for a in ("section", "expert", "tensor"))
    groups = n_section * n_tensor
    me = section * n_tensor + tensor
    rows, width = w.shape
    cols = width // groups
    n_probes = seed_col.shape[0]
    n_tall, n_deep = w_sem.shape
    tall, deep = rows // n_tall, width // n_deep
    n_wide = piece_send.shape[0] // n_tall
    wide = cols // n_wide
    per_layer = groups // layers

    def partner(k, sign):
        return partner_of(n_section, n_tensor, section, tensor, k, sign)

    def remote(src, dst, send, recv, k):
        s, t = partner(k, 1)
        return pltpu.make_async_remote_copy(
            src_ref=src, dst_ref=dst, send_sem=send, recv_sem=recv,
            device_id={"section": s, "tensor": t}, device_id_type=MESH)

    def block_copy(k):
        s, t = partner(k, 1)
        return remote(
            staged.at[s * n_tensor + t], arrived.at[me], send_sem.at[k], recv_sem.at[k], k)

    def piece_copy(h, q):
        s, t = partner(0, 1)
        at = (slice(h * tall, (h + 1) * tall), slice(q * wide, (q + 1) * wide))
        return remote(
            staged.at[(s * n_tensor + t, *at)], arrived.at[(me, *at)],
            piece_send.at[h * n_wide + q], piece_recv.at[h * n_wide + q], 0)

    def scale_copy():
        return remote(own_scale, first_scale, scale_sem.at[0], scale_sem.at[1], 0)

    def mean_copy(k):
        return remote(means_ref.at[me], means_ref.at[me], mean_send.at[k], mean_recv.at[k], k)

    def part_copy(k):
        return remote(parts.at[me], parts.at[me], part_send.at[k], part_recv.at[k], k)

    def gain_copy(j):
        return pltpu.make_async_remote_copy(
            src_ref=gains.at[expert], dst_ref=gains.at[expert], send_sem=gain_send.at[j],
            recv_sem=gain_recv.at[j], device_id={"expert": (expert + j + 1) % n_expert},
            device_id_type=MESH)

    def w_copy(h, c):
        at = (pl.ds(h * tall, tall), pl.ds(pl.multiple_of(c * deep, deep), deep))
        return pltpu.make_async_copy(w_hbm.at[(0, *at)], w.at[at], w_sem.at[h, c])

    small = [
        pltpu.make_async_copy(src, dst, small_sem.at[i]) for i, (src, dst) in enumerate((
            (cols_hbm, cols_ref), (gains_hbm, gains.at[expert]), (seeds_hbm, seeds_ref),
            (order_hbm, order_s)))]
    for copy in small:
        copy.start()
    for h in range(n_tall):
        @pl.loop(0, n_deep)
        def _(c):
            w_copy(h, c).start()

    barrier = pltpu.get_barrier_semaphore()

    @pl.loop(0, n_expert - 1)
    def _(j):
        pl.semaphore_signal(
            barrier, inc=1, device_id={"expert": (expert + j + 1) % n_expert},
            device_id_type=MESH)

    @pl.loop(0, groups - 1)
    def _(k):
        s, t = partner(k, 1)
        pl.semaphore_signal(
            barrier, inc=1, device_id={"section": s, "tensor": t}, device_id_type=MESH)

    print_acc[...] = jnp.zeros_like(print_acc)
    small[0].wait()
    s0, t0 = partner(0, 1)
    g0 = s0 * n_tensor + t0

    for q in range(n_wide):
        wanted = cols_ref[:, pl.ds(pl.multiple_of(g0 * cols, cols) + q * wide, wide)]

        @pl.loop(0, n_deep)
        def _(c):
            ids = lax.broadcasted_iota(jnp.int32, (deep, wide), 0)
            onehot[pl.ds(pl.multiple_of(c * deep, deep), deep), :wide] = jnp.where(
                ids == wanted - c * deep, 1.0, 0.0).astype(jnp.bfloat16)

        for h in range(n_tall):
            part = (slice(h * tall, (h + 1) * tall), slice(q * wide, (q + 1) * wide))
            acc[part] = jnp.zeros((tall, wide), jnp.float32)

            @pl.loop(0, n_deep)
            def _(c):
                if q == 0:
                    w_copy(h, c).wait()
                at = pl.ds(pl.multiple_of(c * deep, deep), deep)
                acc[part] += jnp.dot(
                    w[part[0], at], onehot[at, :wide], preferred_element_type=jnp.float32)

            staged[(g0, *part)] = acc[part].astype(jnp.bfloat16)
            if q == 0 and h == 0:
                small[1].wait()
                pl.semaphore_wait(barrier, groups - 1 + n_expert - 1)

                @pl.loop(0, n_expert - 1)
                def _(j):
                    gain_copy(j).start()

            piece_copy(h, q).start()

    @pl.loop(0, n_expert - 1)
    def _(j):
        gain_copy(j).wait()

    total = gains[0]
    for e in range(1, n_expert):
        total = total + gains[e]
    mean = total / n_expert
    means_ref[me] = mean
    own_scale[...] = gains[expert] / mean
    scale[...] = jnp.broadcast_to(own_scale[...], (128, rows)).T
    scale_copy().start()

    @pl.loop(0, groups - 1)
    def _(k):
        mean_copy(k).start()

    def column_probe(g, c):
        ids = g * cols + c * 128 + lax.broadcasted_iota(jnp.int32, (1, 128), 1)
        return probe_values(7919 * (ids + 1))

    for c in range(cols // 128):
        part = slice(c * 128, (c + 1) * 128)
        block = (staged[g0, :, part].astype(jnp.float32) * scale[...]).astype(jnp.bfloat16)
        print_acc[...] += block.astype(jnp.float32) * column_probe(g0, c)

    @pl.loop(1, groups)
    def _(k):
        s, t = partner(k, 1)
        g = s * n_tensor + t
        wanted = cols_ref[:, pl.ds(pl.multiple_of(g * cols, cols), cols)]
        acc[...] = jnp.zeros_like(acc)

        @pl.loop(0, n_deep)
        def _(c):
            ids = lax.broadcasted_iota(jnp.int32, (deep, cols), 0)
            onehot[:deep] = jnp.where(ids == wanted - c * deep, 1.0, 0.0).astype(jnp.bfloat16)
            acc[...] += jnp.dot(
                w[:, pl.ds(pl.multiple_of(c * deep, deep), deep)], onehot[:deep],
                preferred_element_type=jnp.float32)

        for c in range(cols // 128):
            part = slice(c * 128, (c + 1) * 128)
            block = (acc[:, part] * scale[...]).astype(jnp.bfloat16)
            staged[g, :, part] = block
            print_acc[...] += block.astype(jnp.float32) * column_probe(g, c)

        @pl.when(k < groups - 2)
        def _():
            block_copy(k).start()

    small[2].wait()
    small[3].wait()
    sums_ref[...] = jnp.zeros_like(sums_ref)
    seeds = seeds_ref[...]
    seed_col[...] = jnp.broadcast_to(
        seeds.astype(jnp.float32), (128, n_probes)).T.astype(jnp.int32)
    for b in range(layers):
        order_ref[b:b + 1, :] = jnp.full((1, 128), order_s[0, b], jnp.int32).astype(jnp.float32)

    def first_row(g):
        return order_s[0, g // per_layer] * (rows * per_layer) + (g % per_layer) * rows

    totals = jnp.sum(print_acc[...], axis=1, keepdims=True)
    row_ids = first_row(me) + lax.broadcasted_iota(jnp.int32, (rows, 128), 0)
    for c in range(n_probes // 128):
        part = slice(c * 128, (c + 1) * 128)
        values = probe_values(seeds[:, part] * (row_ids + 1))
        parts[me, :, part] = jnp.sum(values * totals, axis=0, keepdims=True)

    @pl.loop(0, groups - 1)
    def _(k):
        part_copy(k).start()

    block_copy(groups - 2).start()

    def fill(k, to):
        s, t = partner(k, -1)
        first = first_row(s * n_tensor + t) + 1
        chunk = min(64, n_probes)

        @pl.loop(0, n_probes // chunk)
        def _(r):
            at = pl.ds(pl.multiple_of(r * chunk, chunk), chunk)
            for c in range(rows // 128):
                ids = first + c * 128 + lax.broadcasted_iota(jnp.int32, (1, 128), 1)
                to[at, c * 128:(c + 1) * 128] = probe_values(
                    seed_col[at, :] * ids).astype(jnp.bfloat16)

    def sketch(block):
        sums_ref[...] += jnp.dot(probes[...], block, preferred_element_type=jnp.float32)

    arrived[me] = staged[me]
    fill(groups - 1, probes)
    sketch(staged[me])

    fill(0, probes)
    scale_copy().wait()
    for i in range(n_tall * n_wide):
        piece_copy(i // n_wide, i % n_wide).wait()
    s0, t0 = partner(0, -1)
    first = s0 * n_tensor + t0
    scale[...] = jnp.broadcast_to(first_scale[...], (128, rows)).T
    for c in range(cols // 128):
        part = slice(c * 128, (c + 1) * 128)
        arrived[first, :, part] = (
            arrived[first, :, part].astype(jnp.float32) * scale[...]).astype(jnp.bfloat16)
    sketch(arrived[first])

    @pl.loop(1, groups - 1 - late)
    def _(k):
        s, t = partner(k, -1)
        fill(k, probes)
        block_copy(k).wait_recv()
        sketch(arrived[s * n_tensor + t])

    for j in range(late):
        fill(groups - 1 - late + j, late_probes.at[j])

    @pl.loop(0, groups - 1)
    def _(k):
        part_copy(k).wait()
        mean_copy(k).wait()

    printed = parts[0]
    for g in range(1, groups):
        printed = printed + parts[g]
    print_ref[...] = printed * width ** -0.5

    @pl.loop(groups - 1 - late, groups - 1)
    def _(k):
        block_copy(k).wait_recv()

    @pl.loop(1, groups - 1)
    def _(k):
        block_copy(k).wait_send()


def place(n_section, n_tensor, layers, late,
          order_ref, late_probes, blocks_ref, sums_ref, print_ref, means_ref,
          weights_out, sums_out, print_out, means_out,
          total, block_sem, mean_sem, sum_sem, print_sem):
    section, tensor = (lax.axis_index(a) for a in ("section", "tensor"))
    groups = blocks_ref.shape[0]
    per_layer = groups // layers
    chunk = sums_ref.shape[0] // sum_sem.shape[0]
    order = [jnp.max(order_ref[b:b + 1, :]).astype(jnp.int32) for b in range(layers)]

    def copies(g):
        to = order[g // per_layer] * per_layer + g % per_layer
        return (pltpu.make_async_copy(blocks_ref.at[g], weights_out.at[to], block_sem.at[g]),
                pltpu.make_async_copy(means_ref.at[g], means_out.at[to], mean_sem.at[g]))

    def sum_copy(r):
        at = pl.ds(r * chunk, chunk)
        return pltpu.make_async_copy(total.at[at], sums_out.at[at], sum_sem.at[r])

    print_copy = pltpu.make_async_copy(print_ref, print_out, print_sem)

    for g in range(groups):
        for copy in copies(g):
            copy.start()
    print_copy.start()

    for r in range(sum_sem.shape[0]):
        at = slice(r * chunk, (r + 1) * chunk)
        value = sums_ref[at, :]
        for j in range(late):
            s, t = partner_of(n_section, n_tensor, section, tensor, groups - 1 - late + j, -1)
            value += jnp.dot(late_probes[j, at, :], blocks_ref[s * n_tensor + t],
                             preferred_element_type=jnp.float32)
        total[at, :] = value
        sum_copy(r).start()

    for g in range(groups):
        for copy in copies(g):
            copy.wait()
    print_copy.wait()
    for r in range(sum_sem.shape[0]):
        sum_copy(r).wait()


def local(n_section, n_expert, n_tensor, branch_weights, branch_gains, column_order,
          layer_order, probe_seeds):
    _, rows, width = branch_weights.shape
    groups = n_section * n_tensor
    cols = width // groups
    layers = layer_order.shape[0]
    n_probes = probe_seeds.shape[0]
    deep = min(1024, width)
    late = min(LATE, groups - 2)
    n_tall = 2 if rows % 32 == 0 else 1
    n_wide = 2 if cols % 256 == 0 else 1
    f32, bf16 = jnp.float32, jnp.bfloat16
    vmem = pl.BlockSpec(memory_space=pltpu.VMEM)
    hbm = pl.BlockSpec(memory_space=pltpu.HBM)
    dma = pltpu.SemaphoreType.DMA
    arrived, sums, printed, means, late_probes, order = pl.pallas_call(
        functools.partial(exchange, n_section, n_expert, n_tensor, layers, late),
        out_shape=(
            jax.ShapeDtypeStruct((groups, rows, cols), bf16),
            jax.ShapeDtypeStruct((n_probes, cols), f32),
            jax.ShapeDtypeStruct((1, n_probes), f32),
            jax.ShapeDtypeStruct((groups, 1, rows), f32),
            jax.ShapeDtypeStruct((late, n_probes, rows), bf16),
            jax.ShapeDtypeStruct((-(-layers // 8) * 8, 128), f32),
        ),
        in_specs=[hbm] * 5,
        out_specs=(vmem,) * 6,
        scratch_shapes=[
            pltpu.VMEM((rows, width), bf16),
            pltpu.VMEM((groups, rows, cols), bf16),
            pltpu.VMEM((rows, cols), f32),
            pltpu.VMEM((width, cols), bf16),
            pltpu.VMEM((rows, 128), f32),
            pltpu.VMEM((rows, 128), f32),
            pltpu.VMEM((n_probes, 128), jnp.int32),
            pltpu.VMEM((n_probes, rows), bf16),
            pltpu.VMEM((n_expert, 1, rows), f32),
            pltpu.VMEM((groups, 1, n_probes), f32),
            pltpu.VMEM((1, width), jnp.int32),
            pltpu.VMEM((1, n_probes), jnp.int32),
            pltpu.SMEM((1, layers), jnp.int32),
            pltpu.VMEM((1, rows), f32),
            pltpu.VMEM((1, rows), f32),
            dma((n_tall, width // deep)), dma((groups,)), dma((groups,)),
            dma((n_expert,)), dma((n_expert,)), dma((groups,)), dma((groups,)),
            dma((groups,)), dma((groups,)), dma((n_tall * n_wide,)), dma((n_tall * n_wide,)),
            dma((2,)), dma((4,)),
        ],
        compiler_params=pltpu.CompilerParams(
            collective_id=0, has_side_effects=True, vmem_limit_bytes=40 * 2 ** 20),
        name="exchange",
    )(*(pltpu.with_memory_space_constraint(x, pltpu.HBM) for x in (
        layer_order.reshape(1, layers), branch_weights, branch_gains, column_order,
        probe_seeds.reshape(1, n_probes))))

    n_sums = 4 if n_probes % 512 == 0 else 1
    weights, sums, printed, means = pl.pallas_call(
        functools.partial(place, n_section, n_tensor, layers, late),
        in_specs=[vmem] * 6,
        out_specs=(hbm, hbm, hbm, hbm),
        scratch_shapes=[
            pltpu.VMEM((n_probes, cols), f32), dma((groups,)), dma((groups,)), dma((n_sums,)),
            dma(())],
        out_shape=(
            jax.ShapeDtypeStruct((groups, rows, cols), bf16),
            jax.ShapeDtypeStruct((n_probes, cols), f32),
            jax.ShapeDtypeStruct((1, n_probes), f32),
            jax.ShapeDtypeStruct((groups, 1, rows), f32),
        ),
        compiler_params=pltpu.CompilerParams(
            has_side_effects=True, vmem_limit_bytes=16 * 2 ** 20),
        name="place",
    )(order, late_probes, arrived, sums, printed, means)
    return (weights.reshape(1, groups * rows, cols), sums[None], printed,
            means.reshape(groups * rows))


def solution(mesh):
    sizes = mesh.shape
    return jax.shard_map(
        functools.partial(local, sizes["section"], sizes["expert"], sizes["tensor"]),
        mesh=mesh,
        in_specs=(
            P("expert", ("section", "tensor"), None),
            P("expert", ("section", "tensor")),
            P("expert", None),
            P(),
            P(),
        ),
        out_specs=(
            P("expert", None, ("section", "tensor")),
            P("expert", None, ("section", "tensor")),
            P("expert", None),
            P(),
        ),
        check_vma=False,
    )
```

time: 207 us -> 197 us (0.952)
  Pallas kernels: 203 us -> 196 us
  local copies, waits for them, and re-layouts: 2.77 us -> 0 us
    pallas_call x1, Pallas kernels: 198 us -> 191 us  [local(): pl.pallas_call(functools.partial(exchange, n_section, n_expert, n_tensor,...]
    unnamed x8 -> x0, local copies, waits for them, and re-layouts: 2.77 us -> none
where the time goes in v1:
time: 197 us
  Pallas kernels  196 us (99%)
    pallas_call x1, Pallas kernels, local(): pl.pallas_call(functools.partial(exchange, n_section, n_expert, n_tensor,...  191 us
    pallas_call x1, Pallas kernels, local(): pl.pallas_call(functools.partial(place, n_section, n_tensor, layers, late...  5.01 us

profile of v1, /device:TPU:9, one launch (start us, length us, event | category | flops | bytes accessed | tf_op | source)
XLA Modules:
  0.0 196.6 jit_solution(11683715274146404243)
XLA Ops:
  0.6 191.0 %exchange.1 = (bf16[16,512,512]{2,1,0:T(8,128)(2,1)S(1)}, f32[1024,512]{1,0:T(8,128)S(1)}, f32[1,1024]{1,0:T(1,128)S(1)}, f32[16,1,512]{2,1,0:T(1,128)S(1)}, bf1...) custom-call(s32[1,4]{1,0:T(1,128)} %bitcast.6, bf16[1,512,8192]{2,1,0:T(8,128)(2,1)} %w_hbm.1, f32[1,512]{1,0:T(1,128)} %gains_hbm.1, ...), custom_call_target="tpu_custom_call" | custom-call | tf_op jit(solution)/shard_map/exchange/pallas_call | solution.py:353
  191.6 5.0 %place.1 = (bf16[16,512,512]{2,1,0:T(8,128)(2,1)}, f32[1024,512]{1,0:T(8,128)}, f32[1,1024]{1,0:T(1,128)}, f32[16,1,512]{2,1,0:T(1,128)}) custom-call(f32[8,128]{1,0:T(8,128)S(1)} %get-tuple-element.14.order_ref, bf16[2,1024,512]{2,1,0:T(8,128)(2,1)S(1)} %get-tuple-element.15.late_probes, bf16[16,512,512]{2,1,0:T(8,128)(2,1)S(1)} %get-tuple-element.16.blocks_ref, ...), custom_call_target="tpu_custom_call" | custom-call | tf_op jit(solution)/shard_map/place/pallas_call | solution.py:394

commit v2 on v1

--- a/solution.py
+++ b/solution.py
@@ -8,7 +8,8 @@
 from jax.sharding import PartitionSpec as P
 
 MESH = pl.DeviceIdType.MESH
-LATE = 2
+LATE = 1
+HELD = 3
 
 
 def probe_values(products):
@@ -19,9 +20,19 @@
     return (digits - 255).astype(jnp.float32) * (1.0 / 256.0)
 
 
+def halves(n_tensor):
+    half = n_tensor // 2 if n_tensor % 2 == 0 else n_tensor
+    return half, n_tensor // half
+
+
+def column_spans(cols):
+    if cols % 512:
+        return [(0, cols)]
+    return [(0, cols // 4), (cols // 4, cols // 4), (cols // 2, cols // 2)]
+
+
 def partner_of(n_section, n_tensor, section, tensor, k, sign):
-    half = n_tensor // 2 if n_tensor % 2 == 0 else n_tensor
-    sides = n_tensor // half
+    half, sides = halves(n_tensor)
     m, cross = k // sides, (k + 1) % sides
     j = cross * (m // n_section % half) + (1 - cross) * ((m + 1) % half)
     q = cross * (m % n_section) + (1 - cross) * ((m + 1) // half % n_section)
@@ -35,9 +46,9 @@
     order_hbm, w_hbm, gains_hbm, cols_hbm, seeds_hbm,
     arrived, sums_ref, print_ref, means_ref, late_probes, order_ref,
     w, staged, acc, onehot, scale, print_acc, seed_col, probes, gains, parts,
-    cols_ref, seeds_ref, order_s, own_scale, first_scale,
+    own_part, cols_ref, seeds_ref, order_s, own_scale, first_scale,
     w_sem, send_sem, recv_sem, gain_send, gain_recv, mean_send, mean_recv,
-    part_send, part_recv, piece_send, piece_recv, scale_sem, small_sem,
+    part_send, part_recv, print_send, print_recv, piece_send, piece_recv, scale_sem, small_sem,
 ):
     section, expert, tensor = (lax.axis_index(a) for a in ("section", "expert", "tensor"))
     groups = n_section * n_tensor
@@ -47,9 +58,14 @@
     n_probes = seed_col.shape[0]
     n_tall, n_deep = w_sem.shape
     tall, deep = rows // n_tall, width // n_deep
-    n_wide = piece_send.shape[0] // n_tall
-    wide = cols // n_wide
+    spans = column_spans(cols)
     per_layer = groups // layers
+    half, sides = halves(n_tensor)
+    near = n_section * half
+    rank = section * half + tensor % half
+    _, _, piece = parts.shape
+    owners = n_probes // piece
+    held = max(groups - 1 - HELD, 1)
 
     def partner(k, sign):
         return partner_of(n_section, n_tensor, section, tensor, k, sign)
@@ -67,19 +83,55 @@
 
     def piece_copy(h, q):
         s, t = partner(0, 1)
-        at = (slice(h * tall, (h + 1) * tall), slice(q * wide, (q + 1) * wide))
+        at = (pl.ds(h * tall, tall), pl.ds(*spans[q]))
         return remote(
             staged.at[(s * n_tensor + t, *at)], arrived.at[(me, *at)],
-            piece_send.at[h * n_wide + q], piece_recv.at[h * n_wide + q], 0)
+            piece_send.at[q * n_tall + h], piece_recv.at[q * n_tall + h], 0)
 
     def scale_copy():
         return remote(own_scale, first_scale, scale_sem.at[0], scale_sem.at[1], 0)
 
-    def mean_copy(k):
-        return remote(means_ref.at[me], means_ref.at[me], mean_send.at[k], mean_recv.at[k], k)
+    def nearby(src, dst, send, recv, p):
+        r = (rank + p) % near
+        return pltpu.make_async_remote_copy(
+            src_ref=src, dst_ref=dst, send_sem=send, recv_sem=recv,
+            device_id={"section": r // half, "tensor": tensor // half * half + r % half},
+            device_id_type=MESH)
+
+    mirror = section * n_tensor + (tensor + half) % n_tensor
+
+    def mirror_copy():
+        return pltpu.make_async_remote_copy(
+            src_ref=means_ref.at[me], dst_ref=means_ref.at[me], send_sem=mean_send.at[0],
+            recv_sem=mean_recv.at[0], device_id={"tensor": (tensor + half) % n_tensor},
+            device_id_type=MESH)
+
+    def mean_copy(p):
+        return nearby(means_ref.at[me], means_ref.at[me], mean_send.at[p], mean_recv.at[p], p)
+
+    def relay_copy(p):
+        return nearby(means_ref.at[mirror], means_ref.at[mirror],
+                      mean_send.at[near + p], mean_recv.at[near + p], p)
+
+    def owned(r):
+        return pl.ds(pl.multiple_of(r * piece, piece), piece)
+
+    def when_owner(r, act):
+        if owners == near:
+            act()
+        else:
+            pl.when(r < owners)(act)
 
     def part_copy(k):
-        return remote(parts.at[me], parts.at[me], part_send.at[k], part_recv.at[k], k)
+        s, t = partner(k, 1)
+        r = s * half + t % half
+        return r, remote(own_part.at[:, owned(r % owners)], parts.at[me],
+                         part_send.at[k], part_recv.at[k], k)
+
+    def print_copy(p):
+        at = owned(rank % owners)
+        return nearby(print_ref.at[:, at], print_ref.at[:, at],
+                      print_send.at[p], print_recv.at[p], p)
 
     def gain_copy(j):
         return pltpu.make_async_remote_copy(
@@ -121,17 +173,17 @@
     s0, t0 = partner(0, 1)
     g0 = s0 * n_tensor + t0
 
-    for q in range(n_wide):
-        wanted = cols_ref[:, pl.ds(pl.multiple_of(g0 * cols, cols) + q * wide, wide)]
+    for q, (left, wide) in enumerate(spans):
+        wanted = cols_ref[:, pl.ds(pl.multiple_of(g0 * cols, cols) + left, wide)]
 
         @pl.loop(0, n_deep)
         def _(c):
-            ids = lax.broadcasted_iota(jnp.int32, (deep, wide), 0)
+            ids = lax.broadcasted_iota(jnp.int16, (deep, wide), 0)
             onehot[pl.ds(pl.multiple_of(c * deep, deep), deep), :wide] = jnp.where(
-                ids == wanted - c * deep, 1.0, 0.0).astype(jnp.bfloat16)
+                ids == (wanted - c * deep).astype(jnp.int16), jnp.bfloat16(1), jnp.bfloat16(0))
 
         for h in range(n_tall):
-            part = (slice(h * tall, (h + 1) * tall), slice(q * wide, (q + 1) * wide))
+            part = (slice(h * tall, (h + 1) * tall), slice(left, left + wide))
             acc[part] = jnp.zeros((tall, wide), jnp.float32)
 
             @pl.loop(0, n_deep)
@@ -166,9 +218,12 @@
     scale[...] = jnp.broadcast_to(own_scale[...], (128, rows)).T
     scale_copy().start()
 
-    @pl.loop(0, groups - 1)
-    def _(k):
-        mean_copy(k).start()
+    if sides == 2:
+        mirror_copy().start()
+
+    @pl.loop(1, near)
+    def _(p):
+        mean_copy(p).start()
 
     def column_probe(g, c):
         ids = g * cols + c * 128 + lax.broadcasted_iota(jnp.int32, (1, 128), 1)
@@ -179,8 +234,7 @@
         block = (staged[g0, :, part].astype(jnp.float32) * scale[...]).astype(jnp.bfloat16)
         print_acc[...] += block.astype(jnp.float32) * column_probe(g0, c)
 
-    @pl.loop(1, groups)
-    def _(k):
+    def permute(k):
         s, t = partner(k, 1)
         g = s * n_tensor + t
         wanted = cols_ref[:, pl.ds(pl.multiple_of(g * cols, cols), cols)]
@@ -188,8 +242,9 @@
 
         @pl.loop(0, n_deep)
         def _(c):
-            ids = lax.broadcasted_iota(jnp.int32, (deep, cols), 0)
-            onehot[:deep] = jnp.where(ids == wanted - c * deep, 1.0, 0.0).astype(jnp.bfloat16)
+            ids = lax.broadcasted_iota(jnp.int16, (deep, cols), 0)
+            onehot[:deep] = jnp.where(
+                ids == (wanted - c * deep).astype(jnp.int16), jnp.bfloat16(1), jnp.bfloat16(0))
             acc[...] += jnp.dot(
                 w[:, pl.ds(pl.multiple_of(c * deep, deep), deep)], onehot[:deep],
                 preferred_element_type=jnp.float32)
@@ -200,9 +255,17 @@
             staged[g, :, part] = block
             print_acc[...] += block.astype(jnp.float32) * column_probe(g, c)
 
-        @pl.when(k < groups - 2)
+        @pl.when(k < held)
         def _():
             block_copy(k).start()
+
+    @pl.loop(1, groups - 2)
+    def _(n):
+        permute(n + 2 - 4 * (n % 2) + 3 * ((groups - n) // (groups - 1)))
+
+    @pl.loop(0, 2)
+    def _(i):
+        permute(groups - 3 + 2 * i)
 
     small[2].wait()
     small[3].wait()
@@ -221,13 +284,24 @@
     for c in range(n_probes // 128):
         part = slice(c * 128, (c + 1) * 128)
         values = probe_values(seeds[:, part] * (row_ids + 1))
-        parts[me, :, part] = jnp.sum(values * totals, axis=0, keepdims=True)
+        own_part[:, part] = jnp.sum(values * totals, axis=0, keepdims=True)
 
     @pl.loop(0, groups - 1)
     def _(k):
-        part_copy(k).start()
-
-    block_copy(groups - 2).start()
+        r, copy = part_copy(k)
+        when_owner(r, copy.start)
+
+    if sides == 2:
+        mirror_copy().wait()
+
+        @pl.loop(1, near)
+        def _(p):
+            relay_copy(p).start()
+
+    parts[me] = own_part[:, owned(rank % owners)]
+    @pl.loop(held, groups - 1)
+    def _(k):
+        block_copy(k).start()
 
     def fill(k, to):
         s, t = partner(k, -1)
@@ -251,8 +325,8 @@
 
     fill(0, probes)
     scale_copy().wait()
-    for i in range(n_tall * n_wide):
-        piece_copy(i // n_wide, i % n_wide).wait()
+    for i in range(n_tall * len(spans)):
+        piece_copy(i % n_tall, i // n_tall).wait()
     s0, t0 = partner(0, -1)
     first = s0 * n_tensor + t0
     scale[...] = jnp.broadcast_to(first_scale[...], (128, rows)).T
@@ -262,25 +336,48 @@
             arrived[first, :, part].astype(jnp.float32) * scale[...]).astype(jnp.bfloat16)
     sketch(arrived[first])
 
-    @pl.loop(1, groups - 1 - late)
-    def _(k):
+    def catch(k):
         s, t = partner(k, -1)
         fill(k, probes)
         block_copy(k).wait_recv()
         sketch(arrived[s * n_tensor + t])
 
+    middle = max(min(held, groups - 1 - late), 1)
+    pl.loop(1, middle)(catch)
+
+    @pl.loop(0, groups - 1)
+    def _(k):
+        r, copy = part_copy(k)
+        when_owner(r, copy.wait_send)
+
+    def gather():
+        @pl.loop(0, groups - 1)
+        def _(k):
+            part_copy(k)[1].wait_recv()
+
+        printed = parts[0]
+        for g in range(1, groups):
+            printed = printed + parts[g]
+        print_ref[:, owned(rank % owners)] = printed * width ** -0.5
+
+        @pl.loop(1, near)
+        def _(p):
+            print_copy(p).start()
+
+    when_owner(rank, gather)
+
+    pl.loop(middle, groups - 1 - late)(catch)
+
     for j in range(late):
         fill(groups - 1 - late + j, late_probes.at[j])
 
-    @pl.loop(0, groups - 1)
-    def _(k):
-        part_copy(k).wait()
-        mean_copy(k).wait()
-
-    printed = parts[0]
-    for g in range(1, groups):
-        printed = printed + parts[g]
-    print_ref[...] = printed * width ** -0.5
+    @pl.loop(1, near)
+    def _(p):
+        mean_copy(p).wait()
+        if sides == 2:
+            relay_copy(p).wait()
+        when_owner((rank + near - p) % near, print_copy(p).wait_recv)
+        when_owner(rank, print_copy(p).wait_send)
 
     @pl.loop(groups - 1 - late, groups - 1)
     def _(k):
@@ -345,7 +442,9 @@
     deep = min(1024, width)
     late = min(LATE, groups - 2)
     n_tall = 2 if rows % 32 == 0 else 1
-    n_wide = 2 if cols % 256 == 0 else 1
+    n_pieces = n_tall * len(column_spans(cols))
+    near = n_section * halves(n_tensor)[0]
+    owners = near if n_probes % (128 * near) == 0 else min(near, n_probes // 128)
     f32, bf16 = jnp.float32, jnp.bfloat16
     vmem = pl.BlockSpec(memory_space=pltpu.VMEM)
     hbm = pl.BlockSpec(memory_space=pltpu.HBM)
@@ -372,16 +471,17 @@
             pltpu.VMEM((n_probes, 128), jnp.int32),
             pltpu.VMEM((n_probes, rows), bf16),
             pltpu.VMEM((n_expert, 1, rows), f32),
-            pltpu.VMEM((groups, 1, n_probes), f32),
+            pltpu.VMEM((groups, 1, n_probes // owners), f32),
+            pltpu.VMEM((1, n_probes), f32),
             pltpu.VMEM((1, width), jnp.int32),
             pltpu.VMEM((1, n_probes), jnp.int32),
             pltpu.SMEM((1, layers), jnp.int32),
             pltpu.VMEM((1, rows), f32),
             pltpu.VMEM((1, rows), f32),
             dma((n_tall, width // deep)), dma((groups,)), dma((groups,)),
-            dma((n_expert,)), dma((n_expert,)), dma((groups,)), dma((groups,)),
-            dma((groups,)), dma((groups,)), dma((n_tall * n_wide,)), dma((n_tall * n_wide,)),
-            dma((2,)), dma((4,)),
+            dma((n_expert,)), dma((n_expert,)), dma((2 * near,)), dma((2 * near,)),
+            dma((groups,)), dma((groups,)), dma((near,)), dma((near,)),
+            dma((n_pieces,)), dma((n_pieces,)), dma((2,)), dma((4,)),
         ],
         compiler_params=pltpu.CompilerParams(
             collective_id=0, has_side_effects=True, vmem_limit_bytes=40 * 2 ** 20),
@@ -390,7 +490,7 @@
         layer_order.reshape(1, layers), branch_weights, branch_gains, column_order,
         probe_seeds.reshape(1, n_probes))))
 
-    n_sums = 4 if n_probes % 512 == 0 else 1
+    n_sums = 2 if n_probes % 512 == 0 else 1
     weights, sums, printed, means = pl.pallas_call(
         functools.partial(place, n_section, n_tensor, layers, late),
         in_specs=[vmem] * 6,

time: 197 us -> 194 us (0.985)
  Pallas kernels: 196 us -> 194 us
    pallas_call x1, Pallas kernels: 191 us -> 189 us  [local(): pl.pallas_call(functools.partial(exchange, n_section, n_expert, n_tensor,...]
where the time goes in v2:
time: 194 us
  Pallas kernels  194 us (100%)
    pallas_call x1, Pallas kernels, local(): pl.pallas_call(functools.partial(exchange, n_section, n_expert, n_tensor,...  189 us
    pallas_call x1, Pallas kernels, local(): pl.pallas_call(functools.partial(place, n_section, n_tensor, layers, late...  4.77 us

profile of v2, /device:TPU:9, one launch (start us, length us, event | category | flops | bytes accessed | tf_op | source)
XLA Modules:
  0.0 194.2 jit_solution(6901620697200183401)
XLA Ops:
  0.6 188.8 %exchange.1 = (bf16[16,512,512]{2,1,0:T(8,128)(2,1)S(1)}, f32[1024,512]{1,0:T(8,128)S(1)}, f32[1,1024]{1,0:T(1,128)S(1)}, f32[16,1,512]{2,1,0:T(1,128)S(1)}, bf1...) custom-call(s32[1,4]{1,0:T(1,128)} %bitcast.6, bf16[1,512,8192]{2,1,0:T(8,128)(2,1)} %w_hbm.1, f32[1,512]{1,0:T(1,128)} %gains_hbm.1, ...), custom_call_target="tpu_custom_call" | custom-call | tf_op jit(solution)/shard_map/exchange/pallas_call | solution.py:452
  189.5 4.8 %place.1 = (bf16[16,512,512]{2,1,0:T(8,128)(2,1)}, f32[1024,512]{1,0:T(8,128)}, f32[1,1024]{1,0:T(1,128)}, f32[16,1,512]{2,1,0:T(1,128)}) custom-call(f32[8,128]{1,0:T(8,128)S(1)} %get-tuple-element.14.order_ref, bf16[1,1024,512]{2,1,0:T(8,128)(2,1)S(1)} %get-tuple-element.15.late_probes, bf16[16,512,512]{2,1,0:T(8,128)(2,1)S(1)} %get-tuple-element.16.blocks_ref, ...), custom_call_target="tpu_custom_call" | custom-call | tf_op jit(solution)/shard_map/place/pallas_call | solution.py:494

commit v3 on v2

--- a/solution.py
+++ b/solution.py
@@ -398,10 +398,10 @@
     chunk = sums_ref.shape[0] // sum_sem.shape[0]
     order = [jnp.max(order_ref[b:b + 1, :]).astype(jnp.int32) for b in range(layers)]
 
-    def copies(g):
-        to = order[g // per_layer] * per_layer + g % per_layer
-        return (pltpu.make_async_copy(blocks_ref.at[g], weights_out.at[to], block_sem.at[g]),
-                pltpu.make_async_copy(means_ref.at[g], means_out.at[to], mean_sem.at[g]))
+    def copies(b):
+        at, to = pl.ds(b * per_layer, per_layer), pl.ds(order[b] * per_layer, per_layer)
+        return (pltpu.make_async_copy(blocks_ref.at[at], weights_out.at[to], block_sem.at[b]),
+                pltpu.make_async_copy(means_ref.at[at], means_out.at[to], mean_sem.at[b]))
 
     def sum_copy(r):
         at = pl.ds(r * chunk, chunk)
@@ -409,8 +409,8 @@
 
     print_copy = pltpu.make_async_copy(print_ref, print_out, print_sem)
 
-    for g in range(groups):
-        for copy in copies(g):
+    for b in range(layers):
+        for copy in copies(b):
             copy.start()
     print_copy.start()
 
@@ -424,8 +424,8 @@
         total[at, :] = value
         sum_copy(r).start()
 
-    for g in range(groups):
-        for copy in copies(g):
+    for b in range(layers):
+        for copy in copies(b):
             copy.wait()
     print_copy.wait()
     for r in range(sum_sem.shape[0]):
@@ -496,7 +496,7 @@
         in_specs=[vmem] * 6,
         out_specs=(hbm, hbm, hbm, hbm),
         scratch_shapes=[
-            pltpu.VMEM((n_probes, cols), f32), dma((groups,)), dma((groups,)), dma((n_sums,)),
+            pltpu.VMEM((n_probes, cols), f32), dma((layers,)), dma((layers,)), dma((n_sums,)),
             dma(())],
         out_shape=(
             jax.ShapeDtypeStruct((groups, rows, cols), bf16),

time: 194 us -> 194 us (level)
  no operation moved by 1% of the time
where the time goes in v3:
time: 194 us
  Pallas kernels  193 us (99%)
    pallas_call x1, Pallas kernels, local(): pl.pallas_call(functools.partial(exchange, n_section, n_expert, n_tensor,...  189 us
    pallas_call x1, Pallas kernels, local(): pl.pallas_call(functools.partial(place, n_section, n_tensor, layers, late...  4.54 us

profile of v3, /device:TPU:9, one launch (start us, length us, event | category | flops | bytes accessed | tf_op | source)
XLA Modules:
  0.0 194.0 jit_solution(3155439972046924711)
XLA Ops:
  0.6 188.8 %exchange.1 = (bf16[16,512,512]{2,1,0:T(8,128)(2,1)S(1)}, f32[1024,512]{1,0:T(8,128)S(1)}, f32[1,1024]{1,0:T(1,128)S(1)}, f32[16,1,512]{2,1,0:T(1,128)S(1)}, bf1...) custom-call(s32[1,4]{1,0:T(1,128)} %bitcast.6, bf16[1,512,8192]{2,1,0:T(8,128)(2,1)} %w_hbm.1, f32[1,512]{1,0:T(1,128)} %gains_hbm.1, ...), custom_call_target="tpu_custom_call" | custom-call | tf_op jit(solution)/shard_map/exchange/pallas_call | solution.py:452
  189.5 4.5 %place.1 = (bf16[16,512,512]{2,1,0:T(8,128)(2,1)}, f32[1024,512]{1,0:T(8,128)}, f32[1,1024]{1,0:T(1,128)}, f32[16,1,512]{2,1,0:T(1,128)}) custom-call(f32[8,128]{1,0:T(8,128)S(1)} %get-tuple-element.14.order_ref, bf16[1,1024,512]{2,1,0:T(8,128)(2,1)S(1)} %get-tuple-element.15.late_probes, bf16[16,512,512]{2,1,0:T(8,128)(2,1)S(1)} %get-tuple-element.16.blocks_ref, ...), custom_call_target="tpu_custom_call" | custom-call | tf_op jit(solution)/shard_map/place/pallas_call | solution.py:494
